TPU v7x, 32 devices: a whole 2x2x4 slice. The times are simulated.
32 devices in a mesh: gx: 4 (over z), gy: 8 (over y, x, core).
Axes of the slice: x: 2, y: 2, z: 4, core: 2. Of those that a mesh axis runs over, the one named last changes fastest.
Arguments:
- features: bfloat16 [40960, 2048], P(('gx', 'gy')), may hold values from -6 to 6
- counts: int32 [32], P(('gx', 'gy')), may hold values from 128 to 1280, as said below
- ref_mean: float32 [2048], replicated, may hold values from -6 to 6
- ref_root: float32 [2048, 2048], P('gx', 'gy'), as said below
Outputs:
- mean: float32 [2048], replicated
- root: float32 [2048, 2048], P('gx', 'gy')
- distance: float32 [], replicated
Inputs may be any that keep to these rules, and one draw needn't show every extreme that they name: Entry b counts the valid rows of shard b, which come first in it; a multiple of 128; some shard is full in every draw. `ref_root`: symmetric and positive definite.
All inputs are finite; a program needn't handle non-finite values.
Results may differ from a plain program's by a relative error of at most 0.0015.
The roundings to bfloat16 on the way count: a program that leaves them out, or rounds other values in their place, can miss the bound.
Values may be sent and summed in bfloat16 or wider, within the bound.
A program may use at most 128 MiB of HBM per device.

v0:
```python
import jax
import jax.numpy as jnp
from jax import lax
from jax.sharding import PartitionSpec as P

ITERS = 4


def product(left, right):
    left_half = left.astype(jnp.bfloat16)
    right_half = right.astype(jnp.bfloat16)
    panel = lax.all_gather(left_half, "gy", axis=1, tiled=True)
    return jnp.dot(
        panel,
        lax.all_gather(right_half, "gx", axis=0, tiled=True),
        preferred_element_type=jnp.float32,
    )


def shards(features, counts, ref_mean, ref_root):
    width = features.shape[1]
    slots = features.shape[0]
    rows_x = lax.axis_size("gx")
    cols_y = lax.axis_size("gy")
    tile_rows = width // rows_x
    tile_cols = width // cols_y
    keep = (jnp.arange(slots, dtype=jnp.int32) < counts[0])[:, None]
    masked = jnp.where(keep, features, jnp.zeros_like(features))
    partial_gram = lax.dot_general(
        masked, features, (((0,), (0,)), ((), ())), preferred_element_type=jnp.float32
    )
    column_total = jnp.sum(masked.astype(jnp.float32), axis=0)
    local_count = counts[0].astype(jnp.float32)
    total, count = lax.psum((column_total, local_count), ("gx", "gy"))
    column_block = lax.psum_scatter(partial_gram, "gy", scatter_dimension=1, tiled=True)
    gram_tile = lax.psum_scatter(column_block, "gx", scatter_dimension=0, tiled=True)
    mean = total / count
    row_start = lax.axis_index("gx") * tile_rows
    col_start = lax.axis_index("gy") * tile_cols
    mean_rows = lax.dynamic_slice_in_dim(mean, row_start, tile_rows, 0)
    mean_cols = lax.dynamic_slice_in_dim(mean, col_start, tile_cols, 0)
    cov_tile = (gram_tile - count * mean_rows[:, None] * mean_cols[None, :]) / (count - 1.0)
    row_ids = jnp.arange(tile_rows, dtype=jnp.int32) + row_start
    col_ids = jnp.arange(tile_cols, dtype=jnp.int32) + col_start
    identity_tile = (row_ids[:, None] == col_ids[None, :]).astype(jnp.float32)
    half = product(cov_tile, ref_root)
    prod = product(ref_root, half)
    square_sum, cov_trace, root_square = lax.psum(
        (jnp.sum(prod * prod), jnp.sum(cov_tile * identity_tile), jnp.sum(ref_root * ref_root)),
        ("gx", "gy"),
    )
    scale = jnp.sqrt(square_sum + 1.0)
    current = prod / scale
    partner = identity_tile
    for step in range(ITERS):
        middle = 1.5 * identity_tile - 0.5 * product(partner, current)
        current, partner = (product(current, middle), product(middle, partner))
    last_trace = lax.psum(jnp.sum(current * identity_tile), ("gx", "gy"))
    root = jnp.sqrt(scale) * current
    distance = (
        jnp.sum((mean - ref_mean) ** 2)
        + cov_trace
        + root_square
        - 2.0 * jnp.sqrt(scale) * last_trace
    ) / 64.0
    return (mean, root, distance)


def solution(mesh):
    return jax.shard_map(
        shards,
        mesh=mesh,
        in_specs=(P(("gx", "gy"), None), P(("gx", "gy")), P(), P("gx", "gy")),
        out_specs=(P(), P("gx", "gy"), P()),
        check_vma=False,
    )
```

profile of v0, /device:TPU:0, one launch (start us, length us, event | category | flops | bytes accessed | tf_op | source)
XLA Modules:
  0.0 1031.6 jit_solution(1172393237996310174)
XLA Ops:
  7.9 18.1 %fusion = f32[2048,2048]{1,0:T(8,128)} fusion(bf16[1280,2048]{1,0:T(8,128)(2,1)} %param.4, pred[1280]{0:T(1024)(128)(4,1)S(1)} %iota_compare_fusion), kind=kOutput, calls=%fused_computation.1 | convolution fusion | flops 10740039680 | bytes 22021376 | tf_op jit(solution)/shard_map/dot_general | solution.py:29
  26.1 118.8 %reduce-scatter.3.cloned.1.call-done = f32[2048,256]{1,0:T(8,128)} async-done(((f32[2048,2048]{1,0:T(8,128)}), f32[2048,256]{1,0:T(8,128)}) %reduce-scatter.3.cloned.1.call-update) | async-done | bytes 2097168 | tf_op jit(solution)/shard_map/reduce_scatter | solution.py:35
  144.9 1.4 multiply_reduce_fusion
  146.4 3.6 convert_reduce_fusion
  150.0 42.2 %all-reduce.1 = (f32[2048]{0:T(1024)S(1)}, f32[]{:T(128)}) all-reduce(f32[2048]{0:T(1024)S(1)} %convert_reduce_fusion, f32[]{:T(128)S(6)} %convert_element_type.69), channel_id=1, replica_groups=mesh['gx'=4,'gy'=8] {'gx','gy'}, use_global_device_ids=true, to_apply=%region_1.2 | all-reduce | flops 2049 | bytes 16392 | tf_op jit(solution)/shard_map/psum | solution.py:34
  192.9 1.3 multiply_reduce_fusion.2
  195.0 1.9 fusion.16
  197.5 23.1 %all-gather.29.cloned.1.call-done = bf16[2048,256]{1,0:T(8,128)(2,1)} async-done(((bf16[512,256]{1,0:T(8,128)(2,1)}), bf16[2048,256]{1,0:T(8,128)(2,1)}) %all-gather.29.cloned.1.call-update) | async-done | bytes 1048592 | tf_op jit(solution)/shard_map/all_gather | solution.py:15
  220.6 29.8 %all-gather.27.cloned.1.call-done = bf16[512,2048]{1,0:T(8,128)(2,1)} async-done(((bf16[512,256]{1,0:T(8,128)(2,1)}), bf16[512,2048]{1,0:T(8,128)(2,1)}) %all-gather.27.cloned.1.call-update) | async-done | bytes 2097168 | tf_op jit(solution)/shard_map/all_gather | solution.py:12
  250.4 3.3 convolution_convert_fusion.6
  253.8 0.8 fusion.12
  254.7 25.6 %all-gather.33.cloned.1.call-done = bf16[512,2048]{1,0:T(8,128)(2,1)} async-done(((bf16[512,256]{1,0:T(8,128)(2,1)}), bf16[512,2048]{1,0:T(8,128)(2,1)}) %all-gather.33.cloned.1.call-update) | async-done | bytes 2097168 | tf_op jit(solution)/shard_map/all_gather | solution.py:12
  280.3 30.0 %all-gather.31.cloned.1.call-done = bf16[2048,256]{1,0:T(8,128)(2,1)} async-done(((bf16[512,256]{1,0:T(8,128)(2,1)}), bf16[2048,256]{1,0:T(8,128)(2,1)}) %all-gather.31.cloned.1.call-update) | async-done | bytes 1048592 | tf_op jit(solution)/shard_map/all_gather | solution.py:15
  310.3 3.3 multiply_reduce_fusion.1
  313.6 40.4 %psum.44 = f32[]{:T(128)} all-reduce(f32[]{:T(128)} %get-tuple-element.15), channel_id=1, replica_groups=mesh['gx'=4,'gy'=8] {'gx','gy'}, use_global_device_ids=true, to_apply=%region_6.7 | all-reduce | flops 1 | bytes 8 | tf_op jit(solution)/shard_map/psum | solution.py:48
  355.5 27.4 %all-gather.39.cloned.1.call-done = bf16[2048,256]{0,1:T(8,128)(2,1)} async-done(((bf16[512,256]{0,1:T(8,128)(2,1)}), bf16[2048,256]{0,1:T(8,128)(2,1)}) %all-gather.39.cloned.1.call-update) | async-done | bytes 1048592 | tf_op jit(solution)/shard_map/all_gather | solution.py:15
  383.0 3.3 fusion.8
  388.5 25.4 %all-gather.41.cloned.1.call-done = bf16[2048,256]{1,0:T(8,128)(2,1)} async-done(((bf16[512,256]{1,0:T(8,128)(2,1)}), bf16[2048,256]{1,0:T(8,128)(2,1)}) %all-gather.41.cloned.1.call-update) | async-done | bytes 1048592 | tf_op jit(solution)/shard_map/all_gather | solution.py:15
  413.8 29.5 %all-gather.35.cloned.1.call-done = bf16[512,2048]{0,1:T(8,128)(2,1)} async-done(((bf16[512,256]{0,1:T(8,128)(2,1)}), bf16[512,2048]{0,1:T(8,128)(2,1)}) %all-gather.35.cloned.1.call-update) | async-done | bytes 2097168 | tf_op jit(solution)/shard_map/all_gather | solution.py:12
  443.3 3.3 convolution_convert_fusion.5
  446.7 26.2 %all-gather.47.cloned.1.call-done = bf16[2048,256]{1,0:T(8,128)(2,1)} async-done(((bf16[512,256]{1,0:T(8,128)(2,1)}), bf16[2048,256]{1,0:T(8,128)(2,1)}) %all-gather.47.cloned.1.call-update) | async-done | bytes 1048592 | tf_op jit(solution)/shard_map/all_gather | solution.py:15
  472.9 29.2 %all-gather.45.cloned.1.call-done = bf16[512,2048]{1,0:T(8,128)(2,1)} async-done(((bf16[512,256]{1,0:T(8,128)(2,1)}), bf16[512,2048]{1,0:T(8,128)(2,1)}) %all-gather.45.cloned.1.call-update) | async-done | bytes 2097168 | tf_op jit(solution)/shard_map/all_gather | solution.py:12
  502.2 3.3 convolution_convert_fusion.4
  506.1 26.2 %all-gather.51.cloned.1.call-done = bf16[2048,256]{1,0:T(8,128)(2,1)} async-done(((bf16[512,256]{1,0:T(8,128)(2,1)}), bf16[2048,256]{1,0:T(8,128)(2,1)}) %all-gather.51.cloned.1.call-update) | async-done | bytes 1048592 | tf_op jit(solution)/shard_map/all_gather | solution.py:15
  532.3 29.2 %all-gather.49.cloned.1.call-done = bf16[512,2048]{1,0:T(8,128)(2,1)} async-done(((bf16[512,256]{1,0:T(8,128)(2,1)}), bf16[512,2048]{1,0:T(8,128)(2,1)}) %all-gather.49.cloned.1.call-update) | async-done | bytes 2097168 | tf_op jit(solution)/shard_map/all_gather | solution.py:12
  561.6 3.3 fusion.9
  566.1 25.9 %all-gather.43.cloned.1.call-done = bf16[512,2048]{1,0:T(8,128)(2,1)} async-done(((bf16[512,256]{1,0:T(8,128)(2,1)}), bf16[512,2048]{1,0:T(8,128)(2,1)}) %all-gather.43.cloned.1.call-update) | async-done | bytes 2097168 | tf_op jit(solution)/shard_map/all_gather | solution.py:12
  592.0 29.4 %all-gather.53.cloned.1.call-done = bf16[2048,256]{1,0:T(8,128)(2,1)} async-done(((bf16[512,256]{1,0:T(8,128)(2,1)}), bf16[2048,256]{1,0:T(8,128)(2,1)}) %all-gather.53.cloned.1.call-update) | async-done | bytes 1048592 | tf_op jit(solution)/shard_map/all_gather | solution.py:15
  621.4 3.3 convolution_convert_fusion.3
  624.8 25.5 %all-gather.59.cloned.1.call-done = bf16[2048,256]{1,0:T(8,128)(2,1)} async-done(((bf16[512,256]{1,0:T(8,128)(2,1)}), bf16[2048,256]{1,0:T(8,128)(2,1)}) %all-gather.59.cloned.1.call-update) | async-done | bytes 1048592 | tf_op jit(solution)/shard_map/all_gather | solution.py:15
  650.2 29.2 %all-gather.57.cloned.1.call-done = bf16[512,2048]{1,0:T(8,128)(2,1)} async-done(((bf16[512,256]{1,0:T(8,128)(2,1)}), bf16[512,2048]{1,0:T(8,128)(2,1)}) %all-gather.57.cloned.1.call-update) | async-done | bytes 2097168 | tf_op jit(solution)/shard_map/all_gather | solution.py:12
  679.5 3.3 convolution_convert_fusion.2
  683.6 26.1 %all-gather.63.cloned.1.call-done = bf16[2048,256]{1,0:T(8,128)(2,1)} async-done(((bf16[512,256]{1,0:T(8,128)(2,1)}), bf16[2048,256]{1,0:T(8,128)(2,1)}) %all-gather.63.cloned.1.call-update) | async-done | bytes 1048592 | tf_op jit(solution)/shard_map/all_gather | solution.py:15
  709.6 29.2 %all-gather.61.cloned.1.call-done = bf16[512,2048]{1,0:T(8,128)(2,1)} async-done(((bf16[512,256]{1,0:T(8,128)(2,1)}), bf16[512,2048]{1,0:T(8,128)(2,1)}) %all-gather.61.cloned.1.call-update) | async-done | bytes 2097168 | tf_op jit(solution)/shard_map/all_gather | solution.py:12
  738.9 3.3 fusion.10
  743.5 25.9 %all-gather.55.cloned.1.call-done = bf16[512,2048]{1,0:T(8,128)(2,1)} async-done(((bf16[512,256]{1,0:T(8,128)(2,1)}), bf16[512,2048]{1,0:T(8,128)(2,1)}) %all-gather.55.cloned.1.call-update) | async-done | bytes 2097168 | tf_op jit(solution)/shard_map/all_gather | solution.py:12
  769.5 29.6 %all-gather.65.cloned.1.call-done = bf16[2048,256]{1,0:T(8,128)(2,1)} async-done(((bf16[512,256]{1,0:T(8,128)(2,1)}), bf16[2048,256]{1,0:T(8,128)(2,1)}) %all-gather.65.cloned.1.call-update) | async-done | bytes 1048592 | tf_op jit(solution)/shard_map/all_gather | solution.py:15
  799.1 3.3 convolution_convert_fusion.1
  802.4 25.6 %all-gather.71.cloned.1.call-done = bf16[2048,256]{1,0:T(8,128)(2,1)} async-done(((bf16[512,256]{1,0:T(8,128)(2,1)}), bf16[2048,256]{1,0:T(8,128)(2,1)}) %all-gather.71.cloned.1.call-update) | async-done | bytes 1048592 | tf_op jit(solution)/shard_map/all_gather | solution.py:15
  828.0 29.2 %all-gather.69.cloned.1.call-done = bf16[512,2048]{1,0:T(8,128)(2,1)} async-done(((bf16[512,256]{1,0:T(8,128)(2,1)}), bf16[512,2048]{1,0:T(8,128)(2,1)}) %all-gather.69.cloned.1.call-update) | async-done | bytes 2097168 | tf_op jit(solution)/shard_map/all_gather | solution.py:12
  857.3 3.3 convolution_convert_fusion
  861.2 26.2 %all-gather.75.cloned.1.call-done = bf16[2048,256]{1,0:T(8,128)(2,1)} async-done(((bf16[512,256]{1,0:T(8,128)(2,1)}), bf16[2048,256]{1,0:T(8,128)(2,1)}) %all-gather.75.cloned.1.call-update) | async-done | bytes 1048592 | tf_op jit(solution)/shard_map/all_gather | solution.py:15
  887.4 29.2 %all-gather.73.cloned.1.call-done = bf16[512,2048]{1,0:T(8,128)(2,1)} async-done(((bf16[512,256]{1,0:T(8,128)(2,1)}), bf16[512,2048]{1,0:T(8,128)(2,1)}) %all-gather.73.cloned.1.call-update) | async-done | bytes 2097168 | tf_op jit(solution)/shard_map/all_gather | solution.py:12
  916.7 3.3 fusion.11
  920.0 27.1 %all-gather.67.cloned.1.call-done = bf16[512,2048]{1,0:T(8,128)(2,1)} async-done(((bf16[512,256]{1,0:T(8,128)(2,1)}), bf16[512,2048]{1,0:T(8,128)(2,1)}) %all-gather.67.cloned.1.call-update) | async-done | bytes 2097168 | tf_op jit(solution)/shard_map/all_gather | solution.py:12
  947.1 29.6 %all-gather.77.cloned.1.call-done = bf16[2048,256]{1,0:T(8,128)(2,1)} async-done(((bf16[512,256]{1,0:T(8,128)(2,1)}), bf16[2048,256]{1,0:T(8,128)(2,1)}) %all-gather.77.cloned.1.call-update) | async-done | bytes 1048592 | tf_op jit(solution)/shard_map/all_gather | solution.py:15
  976.7 4.0 fusion.14
  980.7 40.4 %all-reduce = (f32[]{:T(128)}, f32[]{:T(128)}, f32[]{:T(128)}) all-reduce(f32[]{:T(128)} %get-tuple-element.4, f32[]{:T(128)} %get-tuple-element.12, f32[]{:T(128)} %get-tuple-element.3), channel_id=1, replica_groups=mesh['gx'=4,'gy'=8] {'gx','gy'}, use_global_device_ids=true, to_apply=%region_9.10 | all-reduce | flops 3 | bytes 24 | tf_op jit(solution)/shard_map/psum | solution.py:48
  (72 shorter events, 9.5 us)
Async XLA Ops:
  7.2 137.7 %reduce-scatter.3.cloned.1.call-start = ((), (), s32[]{:S(2)}) async-start(), calls=%async_computation.2 | async-start | bytes 18874368 | tf_op jit(solution)/shard_map/reduce_scatter | solution.py:35
  26.0 118.9 %copy-start = (f32[512,256]{1,0:T(8,128)S(1)}, f32[512,256]{1,0:T(8,128)}, u32[]{:S(2)}) copy-start(f32[512,256]{1,0:T(8,128)} %param.7) | copy-start | bytes 1572868
  26.0 169.0 %reduce-scatter.5.cloned.1.call-start = ((), (), s32[]{:S(2)}) async-start(), calls=%async_computation.3 | async-start | bytes 2621440 | tf_op jit(solution)/shard_map/reduce_scatter | solution.py:36
  144.8 75.8 %all-gather.29.cloned.1.call-start = ((), (), s32[]{:S(2)}) async-start(), calls=%async_computation.5 | async-start | bytes 1310720 | tf_op jit(solution)/shard_map/all_gather | solution.py:15
  146.3 104.1 %all-gather.27.cloned.1.call-start = ((), (), s32[]{:S(2)}) async-start(), calls=%async_computation.4 | async-start | bytes 2359296 | tf_op jit(solution)/shard_map/all_gather | solution.py:12
  146.4 46.5 %copy-start.3 = (f32[2048]{0:T(1024)S(1)}, f32[2048]{0:T(1024)}, u32[]{:S(2)}) copy-start(f32[2048]{0:T(1024)} %param.6) | copy-start | bytes 24580
  194.2 59.5 %copy-start.2 = (f32[2048]{0:T(1024)}, f32[2048]{0:T(1024)S(1)}, u32[]{:S(2)}) copy-start(f32[2048]{0:T(1024)S(1)} %get-tuple-element.11) | copy-start | bytes 24580
  196.9 83.4 %all-gather.33.cloned.1.call-start = ((), (), s32[]{:S(2)}) async-start(), calls=%async_computation.7 | async-start | bytes 2359296 | tf_op jit(solution)/shard_map/all_gather | solution.py:12
  197.5 112.8 %all-gather.31.cloned.1.call-start = ((), (), s32[]{:S(2)}) async-start(), calls=%async_computation.6 | async-start | bytes 1310720 | tf_op jit(solution)/shard_map/all_gather | solution.py:15
  253.7 101.8 %all-gather.37.cloned.1.call-start = ((), (), s32[]{:S(2)}) async-start(), calls=%async_computation.9 | async-start | bytes 2359296 | tf_op jit(solution)/shard_map/all_gather | solution.py:12
  254.7 128.3 %all-gather.39.cloned.1.call-start = ((), (), s32[]{:S(2)}) async-start(), calls=%async_computation.10 | async-start | bytes 1310720 | tf_op jit(solution)/shard_map/all_gather | solution.py:15
  355.5 58.4 %all-gather.41.cloned.1.call-start = ((), (), s32[]{:S(2)}) async-start(), calls=%async_computation.11 | async-start | bytes 1310720 | tf_op jit(solution)/shard_map/all_gather | solution.py:15
  386.3 57.0 %all-gather.35.cloned.1.call-start = ((), (), s32[]{:S(2)}) async-start(), calls=%async_computation.8 | async-start | bytes 2359296 | tf_op jit(solution)/shard_map/all_gather | solution.py:12
  386.9 86.0 %all-gather.47.cloned.1.call-start = ((), (), s32[]{:S(2)}) async-start(), calls=%async_computation.14 | async-start | bytes 1310720 | tf_op jit(solution)/shard_map/all_gather | solution.py:15
  387.7 114.5 %all-gather.45.cloned.1.call-start = ((), (), s32[]{:S(2)}) async-start(), calls=%async_computation.13 | async-start | bytes 2359296 | tf_op jit(solution)/shard_map/all_gather | solution.py:12
  388.2 144.1 %all-gather.51.cloned.1.call-start = ((), (), s32[]{:S(2)}) async-start(), calls=%async_computation.16 | async-start | bytes 1310720 | tf_op jit(solution)/shard_map/all_gather | solution.py:15
  446.7 114.9 %all-gather.49.cloned.1.call-start = ((), (), s32[]{:S(2)}) async-start(), calls=%async_computation.15 | async-start | bytes 2359296 | tf_op jit(solution)/shard_map/all_gather | solution.py:12
  505.5 86.5 %all-gather.43.cloned.1.call-start = ((), (), s32[]{:S(2)}) async-start(), calls=%async_computation.12 | async-start | bytes 2359296 | tf_op jit(solution)/shard_map/all_gather | solution.py:12
  506.1 115.4 %all-gather.53.cloned.1.call-start = ((), (), s32[]{:S(2)}) async-start(), calls=%async_computation.17 | async-start | bytes 1310720 | tf_op jit(solution)/shard_map/all_gather | solution.py:15
  564.9 85.4 %all-gather.59.cloned.1.call-start = ((), (), s32[]{:S(2)}) async-start(), calls=%async_computation.20 | async-start | bytes 1310720 | tf_op jit(solution)/shard_map/all_gather | solution.py:15
  565.5 114.0 %all-gather.57.cloned.1.call-start = ((), (), s32[]{:S(2)}) async-start(), calls=%async_computation.19 | async-start | bytes 2359296 | tf_op jit(solution)/shard_map/all_gather | solution.py:12
  566.0 143.6 %all-gather.63.cloned.1.call-start = ((), (), s32[]{:S(2)}) async-start(), calls=%async_computation.22 | async-start | bytes 1310720 | tf_op jit(solution)/shard_map/all_gather | solution.py:15
  624.7 114.1 %all-gather.61.cloned.1.call-start = ((), (), s32[]{:S(2)}) async-start(), calls=%async_computation.21 | async-start | bytes 2359296 | tf_op jit(solution)/shard_map/all_gather | solution.py:12
  682.8 86.7 %all-gather.55.cloned.1.call-start = ((), (), s32[]{:S(2)}) async-start(), calls=%async_computation.18 | async-start | bytes 2359296 | tf_op jit(solution)/shard_map/all_gather | solution.py:12
  683.5 115.5 %all-gather.65.cloned.1.call-start = ((), (), s32[]{:S(2)}) async-start(), calls=%async_computation.23 | async-start | bytes 1310720 | tf_op jit(solution)/shard_map/all_gather | solution.py:15
  742.2 85.8 %all-gather.71.cloned.1.call-start = ((), (), s32[]{:S(2)}) async-start(), calls=%async_computation.26 | async-start | bytes 1310720 | tf_op jit(solution)/shard_map/all_gather | solution.py:15
  742.9 114.3 %all-gather.69.cloned.1.call-start = ((), (), s32[]{:S(2)}) async-start(), calls=%async_computation.25 | async-start | bytes 2359296 | tf_op jit(solution)/shard_map/all_gather | solution.py:12
  743.5 143.9 %all-gather.75.cloned.1.call-start = ((), (), s32[]{:S(2)}) async-start(), calls=%async_computation.28 | async-start | bytes 1310720 | tf_op jit(solution)/shard_map/all_gather | solution.py:15
  802.3 114.3 %all-gather.73.cloned.1.call-start = ((), (), s32[]{:S(2)}) async-start(), calls=%async_computation.27 | async-start | bytes 2359296 | tf_op jit(solution)/shard_map/all_gather | solution.py:12
  860.5 86.5 %all-gather.67.cloned.1.call-start = ((), (), s32[]{:S(2)}) async-start(), calls=%async_computation.24 | async-start | bytes 2359296 | tf_op jit(solution)/shard_map/all_gather | solution.py:12
  861.1 115.5 %copy-start.1 = (f32[512,256]{1,0:T(8,128)S(1)}, f32[512,256]{1,0:T(8,128)}, u32[]{:S(2)}) copy-start(f32[512,256]{1,0:T(8,128)} %reduce-scatter.5.cloned.1.call-done) | copy-start | bytes 1572868
  861.2 115.5 %all-gather.77.cloned.1.call-start = ((), (), s32[]{:S(2)}) async-start(), calls=%async_computation.29 | async-start | bytes 1310720 | tf_op jit(solution)/shard_map/all_gather | solution.py:15
Sparse Core Ops, SparseCore 0:
  26.1 118.6 reduce-scatter.2
  147.1 44.6 reduce-scatter.4
  193.4 27.1 all-gather.28
  222.9 27.4 all-gather.26
  252.2 28.0 all-gather.32
  282.3 27.9 all-gather.30
  312.2 27.6 all-gather.36
  355.6 27.3 all-gather.38
  386.5 27.3 all-gather.40
  416.2 27.1 all-gather.34
  444.9 27.9 all-gather.46
  474.7 27.4 all-gather.44
  504.3 27.9 all-gather.50
  534.1 27.4 all-gather.48
  563.9 28.0 all-gather.42
  593.4 27.9 all-gather.52
  622.9 27.3 all-gather.58
  652.0 27.4 all-gather.56
  681.6 27.9 all-gather.62
  711.4 27.4 all-gather.60
  741.3 28.0 all-gather.54
  771.0 27.9 all-gather.64
  800.6 27.3 all-gather.70
  829.8 27.4 all-gather.68
  859.4 27.9 all-gather.74
  889.1 27.4 all-gather.72
  919.0 28.0 all-gather.66
  948.7 27.9 all-gather.76
where the time goes:
time: 1030 us
  waiting for transfers between devices  815 us (79%)
  blocking collectives  123 us (12%)
  matrix products  61.5 us (6%)
  between operations  20.3 us (2%)
  other arithmetic  10.5 us (1%)
    all_gather x13, waiting for transfers between devices, product(): lax.all_gather(right_half, 'gx', axis=0, tiled=True)  350 us
    all_gather x13, waiting for transfers between devices, product(): panel = lax.all_gather(left_half, 'gy', axis=1, tiled=True)  339 us
    reduce_scatter x1, waiting for transfers between devices, shards(): lax.psum_scatter(partial_gram, 'gy', scatter_dimension=1, tiled=True)  119 us
    psum x2, blocking collectives, shards(): lax.psum((jnp.sum(prod * prod), jnp.sum(cov_tile * identity_tile), jnp.su...  80.7 us
    dot_general x13, matrix products, product(): jnp.dot(panel, lax.all_gather(right_half, 'gx', axis=0, tiled=True), pref...  43.4 us
    psum x1, blocking collectives, shards(): total, count = lax.psum((column_total, local_count), ('gx', 'gy'))  42.2 us
  transfers between devices with their start and end apart: 28, of which 26 were waited for; matrix products, arithmetic and copies ran while one was open for 5% of the time, Pallas kernels for 0%

commit v1 on v0

--- a/solution.py
+++ b/solution.py
@@ -6,15 +6,40 @@
 ITERS = 4
 
 
+def vectors_measure(packet, d_out):
+    packet = jnp.moveaxis(packet, 0, d_out)
+    mat_out = packet.shape
+    reached = packet.reshape(
+        *mat_out[:d_out], mat_out[d_out] * mat_out[d_out + 1], *mat_out[d_out + 2 :]
+    )
+    return reached
+
+
+def rest_links(xs, along_axis):
+    odd, opened = (lax.axis_size(along_axis), lax.axis_index(along_axis))
+    block_last, newest = (xs[None], 1)
+    while newest < odd:
+        carry_in = lax.ppermute(
+            block_last, along_axis, perm=list(map(lambda m: (m, m ^ newest), range(odd)))
+        )
+        main = opened & newest == 0
+        block_last = jnp.concatenate(
+            [jnp.where(main, block_last, carry_in), jnp.where(main, carry_in, block_last)]
+        )
+        newest *= 2
+    return block_last
+
+
+def close_the_wall(frame_in, slab_in, axis_k):
+    taken_in = vectors_measure(rest_links(frame_in, slab_in), axis_k)
+    return taken_in
+
+
 def product(left, right):
     left_half = left.astype(jnp.bfloat16)
     right_half = right.astype(jnp.bfloat16)
     panel = lax.all_gather(left_half, "gy", axis=1, tiled=True)
-    return jnp.dot(
-        panel,
-        lax.all_gather(right_half, "gx", axis=0, tiled=True),
-        preferred_element_type=jnp.float32,
-    )
+    return jnp.dot(panel, close_the_wall(right_half, "gx", 0), preferred_element_type=jnp.float32)
 
 
 def shards(features, counts, ref_mean, ref_root):

time: 1030 us -> 776 us (0.75)
  waiting for transfers between devices: 815 us -> 539 us
  starting transfers between devices: 1.3 us -> 23 us
    ppermute x0 -> x26, waiting for transfers between devices: none -> 392 us  [rest_links(): lax.ppermute(block_last, along_axis, perm=list(map(lambda m: (m, m ^ newe...]
    all_gather x13 -> x0, waiting for transfers between devices: 350 us -> none  [product(): lax.all_gather(right_half, 'gx', axis=0, tiled=True)]
    all_gather x13, waiting for transfers between devices: 339 us -> 27.6 us  [product(): panel = lax.all_gather(left_half, 'gy', axis=1, tiled=True)]
    ppermute x0 -> x26, starting transfers between devices: none -> 22.2 us  [rest_links(): lax.ppermute(block_last, along_axis, perm=list(map(lambda m: (m, m ^ newe...]
  transfers between devices with their start and end apart: 28 -> 41, of which waited for: 26 -> 27; matrix products, arithmetic and copies ran while one was open for 5% -> 5% of each run, Pallas kernels for 0% -> 0%
where the time goes in v1:
time: 776 us; the launch traced here: 775 us
  waiting for transfers between devices  539 us (69%)
  blocking collectives  119 us (15%)
  matrix products  55.6 us (7%)
  starting transfers between devices  23 us (3%)
  between operations  20.3 us (3%)
  other arithmetic  17.1 us (2%)
    ppermute x26, waiting for transfers between devices, rest_links(): lax.ppermute(block_last, along_axis, perm=list(map(lambda m: (m, m ^ newe...  392 us
    reduce_scatter x1, waiting for transfers between devices, shards(): lax.psum_scatter(partial_gram, 'gy', scatter_dimension=1, tiled=True)  119 us
    psum x2, blocking collectives, shards(): lax.psum((jnp.sum(prod * prod), jnp.sum(cov_tile * identity_tile), jnp.su...  76.2 us
    psum x1, blocking collectives, shards(): total, count = lax.psum((column_total, local_count), ('gx', 'gy'))  42.7 us
    dot_general x13, matrix products, product(): jnp.dot(panel, close_the_wall(right_half, 'gx', 0), preferred_element_typ...  37.4 us
    all_gather x13, waiting for transfers between devices, product(): panel = lax.all_gather(left_half, 'gy', axis=1, tiled=True)  27.6 us
    ppermute x26, starting transfers between devices, rest_links(): lax.ppermute(block_last, along_axis, perm=list(map(lambda m: (m, m ^ newe...  22.2 us
    dot_general x1, matrix products, shards(): lax.dot_general(masked, features, (((0,), (0,)), ((), ())), preferred_ele...  18.1 us
  transfers between devices with their start and end apart: 41, of which 27 were waited for; matrix products, arithmetic and copies ran while one was open for 5% of the time, Pallas kernels for 0%

profile of v1, /device:TPU:0, one launch (start us, length us, event | category | flops | bytes accessed | tf_op | source)
XLA Modules:
  0.0 774.8 jit_solution(16098159044122355847)
XLA Ops:
  7.9 18.1 %fusion = f32[2048,2048]{1,0:T(8,128)} fusion(bf16[1280,2048]{1,0:T(8,128)(2,1)} %param.4, pred[1280]{0:T(1024)(128)(4,1)S(1)} %iota_compare_fusion), kind=kOutput, calls=%fused_computation.1 | convolution fusion | flops 10740039680 | bytes 22021376 | tf_op jit(solution)/shard_map/dot_general | solution.py:54
  26.1 118.8 %reduce-scatter.3.cloned.1.call-done = f32[2048,256]{1,0:T(8,128)} async-done(((f32[2048,2048]{1,0:T(8,128)}), f32[2048,256]{1,0:T(8,128)}) %reduce-scatter.3.cloned.1.call-update) | async-done | bytes 2097168 | tf_op jit(solution)/shard_map/reduce_scatter | solution.py:60
  145.0 3.7 convert_reduce_fusion
  148.6 42.7 %all-reduce.1 = (f32[2048]{0:T(1024)S(1)}, f32[]{:T(128)}) all-reduce(f32[2048]{0:T(1024)S(1)} %convert_reduce_fusion, f32[]{:T(128)S(6)} %convert_element_type.87), channel_id=1, replica_groups=mesh['gx'=4,'gy'=8] {'gx','gy'}, use_global_device_ids=true, to_apply=%region_1.2 | all-reduce | flops 2049 | bytes 16392 | tf_op jit(solution)/shard_map/psum | solution.py:59
  199.1 7.0 collective-permute-done
  209.2 23.3 %collective-permute-done.1 = bf16[2,512,256]{2,1,0:T(8,128)(2,1)S(1)} collective-permute-done((bf16[2,512,256]{2,1,0:T(8,128)(2,1)S(1)}, bf16[2,512,256]{2,1,0:T(8,128)(2,1)S(1)}, u32[]{:S(2)}, u32[]{:S(2)}) %collective-permute-start.1) | collective-permute-done | bytes 524320 | tf_op jit(solution)/shard_map/ppermute | solution.py:22
  232.7 2.4 fusion.12
  236.1 7.1 collective-permute-done.2
  243.6 24.6 %collective-permute-done.3 = bf16[2,512,256]{2,1,0:T(8,128)(2,1)S(1)} collective-permute-done((bf16[2,512,256]{2,1,0:T(8,128)(2,1)S(1)}, bf16[2,512,256]{2,1,0:T(8,128)(2,1)S(1)}, u32[]{:S(2)}, u32[]{:S(2)}) %collective-permute-start.3) | collective-permute-done | bytes 524320 | tf_op jit(solution)/shard_map/ppermute | solution.py:22
  268.4 3.0 multiply_reduce_fusion.1
  271.4 37.3 %psum.44 = f32[]{:T(128)} all-reduce(f32[]{:T(128)} %get-tuple-element.67), channel_id=1, replica_groups=mesh['gx'=4,'gy'=8] {'gx','gy'}, use_global_device_ids=true, to_apply=%region_6.7 | all-reduce | flops 1 | bytes 8 | tf_op jit(solution)/shard_map/psum | solution.py:73
  309.7 2.9 collective-permute-start.4
  312.6 5.7 collective-permute-done.4
  320.3 22.8 %collective-permute-done.5 = bf16[2,512,256]{2,1,0:T(8,128)(2,1)S(1)} collective-permute-done((bf16[2,512,256]{2,1,0:T(8,128)(2,1)S(1)}, bf16[2,512,256]{2,1,0:T(8,128)(2,1)S(1)}, u32[]{:S(2)}, u32[]{:S(2)}) %collective-permute-start.5) | collective-permute-done | bytes 524320 | tf_op jit(solution)/shard_map/ppermute | solution.py:22
  343.3 3.0 fusion.8
  347.4 7.3 collective-permute-done.8
  355.4 23.9 %collective-permute-done.9 = bf16[2,512,256]{2,1,0:T(8,128)(2,1)S(1)} collective-permute-done((bf16[2,512,256]{2,1,0:T(8,128)(2,1)S(1)}, bf16[2,512,256]{2,1,0:T(8,128)(2,1)S(1)}, u32[]{:S(2)}, u32[]{:S(2)}) %collective-permute-start.9) | collective-permute-done | bytes 524320 | tf_op jit(solution)/shard_map/ppermute | solution.py:22
  379.5 3.0 convolution_convert_fusion.4
  382.7 8.2 %collective-permute-done.6 = bf16[1,512,256]{2,1,0:T(8,128)(2,1)S(1)} collective-permute-done((bf16[1,512,256]{2,1,0:T(8,128)(2,1)S(1)}, bf16[1,512,256]{2,1,0:T(8,128)(2,1)S(1)}, u32[]{:S(2)}, u32[]{:S(2)}) %collective-permute-start.6) | collective-permute-done | bytes 262176 | tf_op jit(solution)/shard_map/ppermute | solution.py:22
  391.4 24.7 %collective-permute-done.7 = bf16[2,512,256]{2,1,0:T(8,128)(2,1)S(1)} collective-permute-done((bf16[2,512,256]{2,1,0:T(8,128)(2,1)S(1)}, bf16[2,512,256]{2,1,0:T(8,128)(2,1)S(1)}, u32[]{:S(2)}, u32[]{:S(2)}) %collective-permute-start.7) | collective-permute-done | bytes 524320 | tf_op jit(solution)/shard_map/ppermute | solution.py:22
  416.4 2.3 convolution_convert_fusion.5
  418.8 8.1 %collective-permute-done.10 = bf16[1,512,256]{2,1,0:T(8,128)(2,1)S(1)} collective-permute-done((bf16[1,512,256]{2,1,0:T(8,128)(2,1)S(1)}, bf16[1,512,256]{2,1,0:T(8,128)(2,1)S(1)}, u32[]{:S(2)}, u32[]{:S(2)}) %collective-permute-start.10) | collective-permute-done | bytes 262176 | tf_op jit(solution)/shard_map/ppermute | solution.py:22
  427.6 24.4 %collective-permute-done.11 = bf16[2,512,256]{2,1,0:T(8,128)(2,1)S(1)} collective-permute-done((bf16[2,512,256]{2,1,0:T(8,128)(2,1)S(1)}, bf16[2,512,256]{2,1,0:T(8,128)(2,1)S(1)}, u32[]{:S(2)}, u32[]{:S(2)}) %collective-permute-start.11) | collective-permute-done | bytes 524320 | tf_op jit(solution)/shard_map/ppermute | solution.py:22
  452.3 3.1 fusion.9
  456.1 8.2 %collective-permute-done.14 = bf16[1,512,256]{2,1,0:T(8,128)(2,1)S(1)} collective-permute-done((bf16[1,512,256]{2,1,0:T(8,128)(2,1)S(1)}, bf16[1,512,256]{2,1,0:T(8,128)(2,1)S(1)}, u32[]{:S(2)}, u32[]{:S(2)}) %collective-permute-start.14) | collective-permute-done | bytes 262176 | tf_op jit(solution)/shard_map/ppermute | solution.py:22
  465.2 24.4 %collective-permute-done.15 = bf16[2,512,256]{2,1,0:T(8,128)(2,1)S(1)} collective-permute-done((bf16[2,512,256]{2,1,0:T(8,128)(2,1)S(1)}, bf16[2,512,256]{2,1,0:T(8,128)(2,1)S(1)}, u32[]{:S(2)}, u32[]{:S(2)}) %collective-permute-start.15) | collective-permute-done | bytes 524320 | tf_op jit(solution)/shard_map/ppermute | solution.py:22
  489.8 3.0 convolution_convert_fusion.2
  493.0 8.2 %collective-permute-done.12 = bf16[1,512,256]{2,1,0:T(8,128)(2,1)S(1)} collective-permute-done((bf16[1,512,256]{2,1,0:T(8,128)(2,1)S(1)}, bf16[1,512,256]{2,1,0:T(8,128)(2,1)S(1)}, u32[]{:S(2)}, u32[]{:S(2)}) %collective-permute-start.12) | collective-permute-done | bytes 262176 | tf_op jit(solution)/shard_map/ppermute | solution.py:22
  502.1 24.4 %collective-permute-done.13 = bf16[2,512,256]{2,1,0:T(8,128)(2,1)S(1)} collective-permute-done((bf16[2,512,256]{2,1,0:T(8,128)(2,1)S(1)}, bf16[2,512,256]{2,1,0:T(8,128)(2,1)S(1)}, u32[]{:S(2)}, u32[]{:S(2)}) %collective-permute-start.13) | collective-permute-done | bytes 524320 | tf_op jit(solution)/shard_map/ppermute | solution.py:22
  526.7 3.0 convolution_convert_fusion.3
  529.9 8.4 %collective-permute-done.16 = bf16[1,512,256]{2,1,0:T(8,128)(2,1)S(1)} collective-permute-done((bf16[1,512,256]{2,1,0:T(8,128)(2,1)}, bf16[1,512,256]{2,1,0:T(8,128)(2,1)S(1)}, u32[]{:S(2)}, u32[]{:S(2)}) %collective-permute-start.16) | collective-permute-done | bytes 262176 | tf_op jit(solution)/shard_map/ppermute | solution.py:22
  540.2 24.3 %collective-permute-done.17 = bf16[2,512,256]{2,1,0:T(8,128)(2,1)S(1)} collective-permute-done((bf16[2,512,256]{2,1,0:T(8,128)(2,1)S(1)}, bf16[2,512,256]{2,1,0:T(8,128)(2,1)S(1)}, u32[]{:S(2)}, u32[]{:S(2)}) %collective-permute-start.17) | collective-permute-done | bytes 524320 | tf_op jit(solution)/shard_map/ppermute | solution.py:22
  564.8 3.1 fusion.10
  568.0 8.4 %collective-permute-done.18 = bf16[1,512,256]{2,1,0:T(8,128)(2,1)S(1)} collective-permute-done((bf16[1,512,256]{2,1,0:T(8,128)(2,1)}, bf16[1,512,256]{2,1,0:T(8,128)(2,1)S(1)}, u32[]{:S(2)}, u32[]{:S(2)}) %collective-permute-start.18) | collective-permute-done | bytes 262176 | tf_op jit(solution)/shard_map/ppermute | solution.py:22
  580.0 22.7 %collective-permute-done.19 = bf16[2,512,256]{2,1,0:T(8,128)(2,1)S(1)} collective-permute-done((bf16[2,512,256]{2,1,0:T(8,128)(2,1)S(1)}, bf16[2,512,256]{2,1,0:T(8,128)(2,1)S(1)}, u32[]{:S(2)}, u32[]{:S(2)}) %collective-permute-start.19) | collective-permute-done | bytes 524320 | tf_op jit(solution)/shard_map/ppermute | solution.py:22
  602.9 2.4 convolution_convert_fusion.1
  605.5 2.4 collective-permute-start.21
  607.9 10.3 %collective-permute-done.22 = bf16[1,512,256]{2,1,0:T(8,128)(2,1)S(1)} collective-permute-done((bf16[1,512,256]{2,1,0:T(8,128)(2,1)S(1)}, bf16[1,512,256]{2,1,0:T(8,128)(2,1)S(1)}, u32[]{:S(2)}, u32[]{:S(2)}) %collective-permute-start.22) | collective-permute-done | bytes 262176 | tf_op jit(solution)/shard_map/ppermute | solution.py:22
  618.5 25.3 %collective-permute-done.21 = bf16[2,512,256]{2,1,0:T(8,128)(2,1)S(1)} collective-permute-done((bf16[2,512,256]{2,1,0:T(8,128)(2,1)S(1)}, bf16[2,512,256]{2,1,0:T(8,128)(2,1)S(1)}, u32[]{:S(2)}, u32[]{:S(2)}) %collective-permute-start.21) | collective-permute-done | bytes 524320 | tf_op jit(solution)/shard_map/ppermute | solution.py:22
  643.8 10.2 %collective-permute-done.23 = bf16[2,512,256]{2,1,0:T(8,128)(2,1)S(1)} collective-permute-done((bf16[2,512,256]{2,1,0:T(8,128)(2,1)S(1)}, bf16[2,512,256]{2,1,0:T(8,128)(2,1)S(1)}, u32[]{:S(2)}, u32[]{:S(2)}) %collective-permute-start.23) | collective-permute-done | bytes 524320 | tf_op jit(solution)/shard_map/ppermute | solution.py:22
  654.3 3.0 convolution_convert_fusion
  658.0 27.3 %all-gather.38.cloned.1.call-done = bf16[512,2048]{1,0:T(8,128)(2,1)} async-done(((bf16[512,256]{1,0:T(8,128)(2,1)}), bf16[512,2048]{1,0:T(8,128)(2,1)}) %all-gather.38.cloned.1.call-update) | async-done | bytes 2097168 | tf_op jit(solution)/shard_map/all_gather | solution.py:41
  685.3 2.3 fusion.13
  689.2 7.0 collective-permute-done.24
  696.3 2.5 collective-permute-start.25
  698.8 22.9 %collective-permute-done.25 = bf16[2,512,256]{2,1,0:T(8,128)(2,1)S(1)} collective-permute-done((bf16[2,512,256]{2,1,0:T(8,128)(2,1)S(1)}, bf16[2,512,256]{2,1,0:T(8,128)(2,1)S(1)}, u32[]{:S(2)}, u32[]{:S(2)}) %collective-permute-start.25) | collective-permute-done | bytes 524320 | tf_op jit(solution)/shard_map/ppermute | solution.py:22
  721.9 3.8 fusion.16
  725.7 38.9 %all-reduce = (f32[]{:T(128)}, f32[]{:T(128)}, f32[]{:T(128)}) all-reduce(f32[]{:T(128)} %get-tuple-element.4, f32[]{:T(128)} %get-tuple-element.38, f32[]{:T(128)} %get-tuple-element.3), channel_id=1, replica_groups=mesh['gx'=4,'gy'=8] {'gx','gy'}, use_global_device_ids=true, to_apply=%region_9.10 | all-reduce | flops 3 | bytes 24 | tf_op jit(solution)/shard_map/psum | solution.py:73
  (151 shorter events, 30.4 us)
Async XLA Ops:
  7.2 137.7 %reduce-scatter.3.cloned.1.call-start = ((), (), s32[]{:S(2)}) async-start(), calls=%async_computation.2 | async-start | bytes 18874368 | tf_op jit(solution)/shard_map/reduce_scatter | solution.py:60
  26.0 168.0 %reduce-scatter.5.cloned.1.call-start = ((), (), s32[]{:S(2)}) async-start(), calls=%async_computation.3 | async-start | bytes 2621440 | tf_op jit(solution)/shard_map/reduce_scatter | solution.py:61
  144.9 87.8 %all-gather.14.cloned.1.call-start = ((), (), s32[]{:S(2)}) async-start(), calls=%async_computation.4 | async-start | bytes 2359296 | tf_op jit(solution)/shard_map/all_gather | solution.py:41
  144.9 47.1 %copy-start.9 = (f32[2048]{0:T(1024)S(1)}, f32[2048]{0:T(1024)}, u32[]{:S(2)}) copy-start(f32[2048]{0:T(1024)} %param.6) | copy-start | bytes 24580
  144.9 51.1 %copy-start.6 = (f32[512,256]{1,0:T(8,128)S(1)}, f32[512,256]{1,0:T(8,128)}, u32[]{:S(2)}) copy-start(f32[512,256]{1,0:T(8,128)} %param.7) | copy-start | bytes 1572868
  193.3 13.9 %copy-start.8 = (f32[2048]{0:T(1024)}, f32[2048]{0:T(1024)S(1)}, u32[]{:S(2)}) copy-start(f32[2048]{0:T(1024)S(1)} %get-tuple-element.11) | copy-start | bytes 24580
  196.0 72.4 %all-gather.16.cloned.1.call-start = ((), (), s32[]{:S(2)}) async-start(), calls=%async_computation.5 | async-start | bytes 2359296 | tf_op jit(solution)/shard_map/all_gather | solution.py:41
  197.4 145.8 %all-gather.20.cloned.1.call-start = ((), (), s32[]{:S(2)}) async-start(), calls=%async_computation.7 | async-start | bytes 2359296 | tf_op jit(solution)/shard_map/all_gather | solution.py:41
  197.5 8.6 %collective-permute-start = (bf16[1,512,256]{2,1,0:T(8,128)(2,1)}, bf16[1,512,256]{2,1,0:T(8,128)(2,1)S(1)}, u32[]{:S(2)}, u32[]{:S(2)}) collective-permute-start(bf16[1,512,256]{2,1,0:T(8,128)(2,1)} %bitcast.81), channel_id=1, source_target_pairs={{0,8},{8,0},{16,24},{24,16},{1,9},{9,1},{17,25},{25,17},{2,10},{10... | collective-permute-start | bytes 786440 | tf_op jit(solution)/shard_map/ppermute | solution.py:22
  207.2 25.3 %collective-permute-start.1 = (bf16[2,512,256]{2,1,0:T(8,128)(2,1)S(1)}, bf16[2,512,256]{2,1,0:T(8,128)(2,1)S(1)}, u32[]{:S(2)}, u32[]{:S(2)}) collective-permute-start(bf16[2,512,256]{2,1,0:T(8,128)(2,1)S(1)} %pad_maximum_fusion.13), channel_id=1, source_target_pairs={{0,16},{8,24},{16,0},{24,8},{1,17},{9,25},{17,1},{25,9},{2,18},{10... | collective-permute-start | bytes 1572872 | tf_op jit(solution)/shard_map/ppermute | solution.py:22
  235.1 8.1 %collective-permute-start.2 = (bf16[1,512,256]{2,1,0:T(8,128)(2,1)S(1)}, bf16[1,512,256]{2,1,0:T(8,128)(2,1)S(1)}, u32[]{:S(2)}, u32[]{:S(2)}) collective-permute-start(bf16[1,512,256]{2,1,0:T(8,128)(2,1)S(1)} %fusion.12), channel_id=1, source_target_pairs={{0,8},{8,0},{16,24},{24,16},{1,9},{9,1},{17,25},{25,17},{2,10},{10... | collective-permute-start | bytes 786440 | tf_op jit(solution)/shard_map/ppermute | solution.py:22
  236.0 143.4 %all-gather.24.cloned.1.call-start = ((), (), s32[]{:S(2)}) async-start(), calls=%async_computation.9 | async-start | bytes 2359296 | tf_op jit(solution)/shard_map/all_gather | solution.py:41
  243.2 25.0 %collective-permute-start.3 = (bf16[2,512,256]{2,1,0:T(8,128)(2,1)S(1)}, bf16[2,512,256]{2,1,0:T(8,128)(2,1)S(1)}, u32[]{:S(2)}, u32[]{:S(2)}) collective-permute-start(bf16[2,512,256]{2,1,0:T(8,128)(2,1)S(1)} %pad_maximum_fusion.14), channel_id=1, source_target_pairs={{0,16},{8,24},{16,0},{24,8},{1,17},{9,25},{17,1},{25,9},{2,18},{10... | collective-permute-start | bytes 1572872 | tf_op jit(solution)/shard_map/ppermute | solution.py:22
  309.7 8.6 %collective-permute-start.4 = (bf16[1,512,256]{2,1,0:T(8,128)(2,1)S(1)}, bf16[1,512,256]{2,1,0:T(8,128)(2,1)S(1)}, u32[]{:S(2)}, u32[]{:S(2)}) collective-permute-start(bf16[1,512,256]{2,1,0:T(8,128)(2,1)S(1)} %fusion.46), channel_id=1, source_target_pairs={{0,8},{8,0},{16,24},{24,16},{1,9},{9,1},{17,25},{25,17},{2,10},{10... | collective-permute-start | bytes 786440 | tf_op jit(solution)/shard_map/ppermute | solution.py:22
  318.4 24.7 %collective-permute-start.5 = (bf16[2,512,256]{2,1,0:T(8,128)(2,1)S(1)}, bf16[2,512,256]{2,1,0:T(8,128)(2,1)S(1)}, u32[]{:S(2)}, u32[]{:S(2)}) collective-permute-start(bf16[2,512,256]{2,1,0:T(8,128)(2,1)S(1)} %pad_maximum_fusion.15), channel_id=1, source_target_pairs={{0,16},{8,24},{16,0},{24,8},{1,17},{9,25},{17,1},{25,9},{2,18},{10... | collective-permute-start | bytes 1572872 | tf_op jit(solution)/shard_map/ppermute | solution.py:22
  346.3 70.1 %all-gather.18.cloned.1.call-start = ((), (), s32[]{:S(2)}) async-start(), calls=%async_computation.6 | async-start | bytes 2359296 | tf_op jit(solution)/shard_map/all_gather | solution.py:41
  347.1 105.1 %all-gather.26.cloned.1.call-start = ((), (), s32[]{:S(2)}) async-start(), calls=%async_computation.10 | async-start | bytes 2359296 | tf_op jit(solution)/shard_map/all_gather | solution.py:41
  347.3 7.4 collective-permute-start.8
  355.0 24.3 %collective-permute-start.9 = (bf16[2,512,256]{2,1,0:T(8,128)(2,1)S(1)}, bf16[2,512,256]{2,1,0:T(8,128)(2,1)S(1)}, u32[]{:S(2)}, u32[]{:S(2)}) collective-permute-start(bf16[2,512,256]{2,1,0:T(8,128)(2,1)S(1)} %pad_maximum_fusion.17), channel_id=1, source_target_pairs={{0,16},{8,24},{16,0},{24,8},{1,17},{9,25},{17,1},{25,9},{2,18},{10... | collective-permute-start | bytes 1572872 | tf_op jit(solution)/shard_map/ppermute | solution.py:22
  382.6 107.2 %all-gather.30.cloned.1.call-start = ((), (), s32[]{:S(2)}) async-start(), calls=%async_computation.12 | async-start | bytes 2359296 | tf_op jit(solution)/shard_map/all_gather | solution.py:41
  382.6 8.3 %collective-permute-start.6 = (bf16[1,512,256]{2,1,0:T(8,128)(2,1)S(1)}, bf16[1,512,256]{2,1,0:T(8,128)(2,1)S(1)}, u32[]{:S(2)}, u32[]{:S(2)}) collective-permute-start(bf16[1,512,256]{2,1,0:T(8,128)(2,1)S(1)} %bitcast.101), channel_id=1, source_target_pairs={{0,8},{8,0},{16,24},{24,16},{1,9},{9,1},{17,25},{25,17},{2,10},{10... | collective-permute-start | bytes 786440 | tf_op jit(solution)/shard_map/ppermute | solution.py:22
  391.0 25.2 %collective-permute-start.7 = (bf16[2,512,256]{2,1,0:T(8,128)(2,1)S(1)}, bf16[2,512,256]{2,1,0:T(8,128)(2,1)S(1)}, u32[]{:S(2)}, u32[]{:S(2)}) collective-permute-start(bf16[2,512,256]{2,1,0:T(8,128)(2,1)S(1)} %pad_maximum_fusion.16), channel_id=1, source_target_pairs={{0,16},{8,24},{16,0},{24,8},{1,17},{9,25},{17,1},{25,9},{2,18},{10... | collective-permute-start | bytes 1572872 | tf_op jit(solution)/shard_map/ppermute | solution.py:22
  418.7 33.5 %copy-start.1 = (bf16[512,256]{1,0:T(8,128)(2,1)}, bf16[512,256]{1,0:T(8,128)(2,1)S(1)}, u32[]{:S(2)}) copy-start(bf16[512,256]{1,0:T(8,128)(2,1)S(1)} %convolution_convert_fusion.5) | copy-start | bytes 786436
  418.7 8.2 %collective-permute-start.10 = (bf16[1,512,256]{2,1,0:T(8,128)(2,1)S(1)}, bf16[1,512,256]{2,1,0:T(8,128)(2,1)S(1)}, u32[]{:S(2)}, u32[]{:S(2)}) collective-permute-start(bf16[1,512,256]{2,1,0:T(8,128)(2,1)S(1)} %bitcast.96), channel_id=1, source_target_pairs={{0,8},{8,0},{16,24},{24,16},{1,9},{9,1},{17,25},{25,17},{2,10},{10... | collective-permute-start | bytes 786440 | tf_op jit(solution)/shard_map/ppermute | solution.py:22
  427.0 25.1 %collective-permute-start.11 = (bf16[2,512,256]{2,1,0:T(8,128)(2,1)S(1)}, bf16[2,512,256]{2,1,0:T(8,128)(2,1)S(1)}, u32[]{:S(2)}, u32[]{:S(2)}) collective-permute-start(bf16[2,512,256]{2,1,0:T(8,128)(2,1)S(1)} %pad_maximum_fusion.18), channel_id=1, source_target_pairs={{0,16},{8,24},{16,0},{24,8},{1,17},{9,25},{17,1},{25,9},{2,18},{10... | collective-permute-start | bytes 1572872 | tf_op jit(solution)/shard_map/ppermute | solution.py:22
  455.4 71.3 %all-gather.22.cloned.1.call-start = ((), (), s32[]{:S(2)}) async-start(), calls=%async_computation.8 | async-start | bytes 2359296 | tf_op jit(solution)/shard_map/all_gather | solution.py:41
  456.0 108.8 %all-gather.32.cloned.1.call-start = ((), (), s32[]{:S(2)}) async-start(), calls=%async_computation.13 | async-start | bytes 2359296 | tf_op jit(solution)/shard_map/all_gather | solution.py:41
  456.0 8.3 %collective-permute-start.14 = (bf16[1,512,256]{2,1,0:T(8,128)(2,1)S(1)}, bf16[1,512,256]{2,1,0:T(8,128)(2,1)S(1)}, u32[]{:S(2)}, u32[]{:S(2)}) collective-permute-start(bf16[1,512,256]{2,1,0:T(8,128)(2,1)S(1)} %bitcast.98), channel_id=1, source_target_pairs={{0,8},{8,0},{16,24},{24,16},{1,9},{9,1},{17,25},{25,17},{2,10},{10... | collective-permute-start | bytes 786440 | tf_op jit(solution)/shard_map/ppermute | solution.py:22
  464.4 25.2 %collective-permute-start.15 = (bf16[2,512,256]{2,1,0:T(8,128)(2,1)S(1)}, bf16[2,512,256]{2,1,0:T(8,128)(2,1)S(1)}, u32[]{:S(2)}, u32[]{:S(2)}) collective-permute-start(bf16[2,512,256]{2,1,0:T(8,128)(2,1)S(1)} %pad_maximum_fusion.20), channel_id=1, source_target_pairs={{0,16},{8,24},{16,0},{24,8},{1,17},{9,25},{17,1},{25,9},{2,18},{10... | collective-permute-start | bytes 1572872 | tf_op jit(solution)/shard_map/ppermute | solution.py:22
  492.9 110.0 %all-gather.28.cloned.1.call-start = ((), (), s32[]{:S(2)}) async-start(), calls=%async_computation.11 | async-start | bytes 2359296 | tf_op jit(solution)/shard_map/all_gather | solution.py:41
  492.9 8.3 %collective-permute-start.12 = (bf16[1,512,256]{2,1,0:T(8,128)(2,1)S(1)}, bf16[1,512,256]{2,1,0:T(8,128)(2,1)S(1)}, u32[]{:S(2)}, u32[]{:S(2)}) collective-permute-start(bf16[1,512,256]{2,1,0:T(8,128)(2,1)S(1)} %bitcast.102), channel_id=1, source_target_pairs={{0,8},{8,0},{16,24},{24,16},{1,9},{9,1},{17,25},{25,17},{2,10},{10... | collective-permute-start | bytes 786440 | tf_op jit(solution)/shard_map/ppermute | solution.py:22
  501.3 25.2 %collective-permute-start.13 = (bf16[2,512,256]{2,1,0:T(8,128)(2,1)S(1)}, bf16[2,512,256]{2,1,0:T(8,128)(2,1)S(1)}, u32[]{:S(2)}, u32[]{:S(2)}) collective-permute-start(bf16[2,512,256]{2,1,0:T(8,128)(2,1)S(1)} %pad_maximum_fusion.19), channel_id=1, source_target_pairs={{0,16},{8,24},{16,0},{24,8},{1,17},{9,25},{17,1},{25,9},{2,18},{10... | collective-permute-start | bytes 1572872 | tf_op jit(solution)/shard_map/ppermute | solution.py:22
  529.8 124.5 %all-gather.36.cloned.1.call-start = ((), (), s32[]{:S(2)}) async-start(), calls=%async_computation.15 | async-start | bytes 2359296 | tf_op jit(solution)/shard_map/all_gather | solution.py:41
  529.8 8.5 %collective-permute-start.16 = (bf16[1,512,256]{2,1,0:T(8,128)(2,1)}, bf16[1,512,256]{2,1,0:T(8,128)(2,1)S(1)}, u32[]{:S(2)}, u32[]{:S(2)}) collective-permute-start(bf16[1,512,256]{2,1,0:T(8,128)(2,1)} %bitcast.100), channel_id=1, source_target_pairs={{0,8},{8,0},{16,24},{24,16},{1,9},{9,1},{17,25},{25,17},{2,10},{10... | collective-permute-start | bytes 786440 | tf_op jit(solution)/shard_map/ppermute | solution.py:22
  539.4 25.2 %collective-permute-start.17 = (bf16[2,512,256]{2,1,0:T(8,128)(2,1)S(1)}, bf16[2,512,256]{2,1,0:T(8,128)(2,1)S(1)}, u32[]{:S(2)}, u32[]{:S(2)}) collective-permute-start(bf16[2,512,256]{2,1,0:T(8,128)(2,1)S(1)} %pad_maximum_fusion.21), channel_id=1, source_target_pairs={{0,16},{8,24},{16,0},{24,8},{1,17},{9,25},{17,1},{25,9},{2,18},{10... | collective-permute-start | bytes 1572872 | tf_op jit(solution)/shard_map/ppermute | solution.py:22
  567.9 10.4 %copy-start = (bf16[512,256]{1,0:T(8,128)(2,1)S(1)}, bf16[512,256]{1,0:T(8,128)(2,1)}, u32[]{:S(2)}) copy-start(bf16[512,256]{1,0:T(8,128)(2,1)} %convolution_convert_fusion.2) | copy-start | bytes 786436
  567.9 117.4 %all-gather.38.cloned.1.call-start = ((), (), s32[]{:S(2)}) async-start(), calls=%async_computation.16 | async-start | bytes 2359296 | tf_op jit(solution)/shard_map/all_gather | solution.py:41
  567.9 8.5 %collective-permute-start.18 = (bf16[1,512,256]{2,1,0:T(8,128)(2,1)}, bf16[1,512,256]{2,1,0:T(8,128)(2,1)S(1)}, u32[]{:S(2)}, u32[]{:S(2)}) collective-permute-start(bf16[1,512,256]{2,1,0:T(8,128)(2,1)} %bitcast.99), channel_id=1, source_target_pairs={{0,8},{8,0},{16,24},{24,16},{1,9},{9,1},{17,25},{25,17},{2,10},{10... | collective-permute-start | bytes 786440 | tf_op jit(solution)/shard_map/ppermute | solution.py:22
  577.5 25.2 %collective-permute-start.19 = (bf16[2,512,256]{2,1,0:T(8,128)(2,1)S(1)}, bf16[2,512,256]{2,1,0:T(8,128)(2,1)S(1)}, u32[]{:S(2)}, u32[]{:S(2)}) collective-permute-start(bf16[2,512,256]{2,1,0:T(8,128)(2,1)S(1)} %pad_maximum_fusion.22), channel_id=1, source_target_pairs={{0,16},{8,24},{16,0},{24,8},{1,17},{9,25},{17,1},{25,9},{2,18},{10... | collective-permute-start | bytes 1572872 | tf_op jit(solution)/shard_map/ppermute | solution.py:22
  578.3 27.1 %collective-permute-start.20 = (bf16[1,512,256]{2,1,0:T(8,128)(2,1)S(1)}, bf16[1,512,256]{2,1,0:T(8,128)(2,1)S(1)}, u32[]{:S(2)}, u32[]{:S(2)}) collective-permute-start(bf16[1,512,256]{2,1,0:T(8,128)(2,1)S(1)} %bitcast.95), channel_id=1, source_target_pairs={{0,8},{8,0},{16,24},{24,16},{1,9},{9,1},{17,25},{25,17},{2,10},{10... | collective-permute-start | bytes 786440 | tf_op jit(solution)/shard_map/ppermute | solution.py:22
  605.3 13.0 %copy-start.2 = (bf16[512,256]{1,0:T(8,128)(2,1)}, bf16[512,256]{1,0:T(8,128)(2,1)S(1)}, u32[]{:S(2)}) copy-start(bf16[512,256]{1,0:T(8,128)(2,1)S(1)} %convolution_convert_fusion.1) | copy-start | bytes 786436
  605.3 12.9 %collective-permute-start.22 = (bf16[1,512,256]{2,1,0:T(8,128)(2,1)S(1)}, bf16[1,512,256]{2,1,0:T(8,128)(2,1)S(1)}, u32[]{:S(2)}, u32[]{:S(2)}) collective-permute-start(bf16[1,512,256]{2,1,0:T(8,128)(2,1)S(1)} %bitcast.97), channel_id=1, source_target_pairs={{0,8},{8,0},{16,24},{24,16},{1,9},{9,1},{17,25},{25,17},{2,10},{10... | collective-permute-start | bytes 786440 | tf_op jit(solution)/shard_map/ppermute | solution.py:22
  605.5 38.2 %collective-permute-start.21 = (bf16[2,512,256]{2,1,0:T(8,128)(2,1)S(1)}, bf16[2,512,256]{2,1,0:T(8,128)(2,1)S(1)}, u32[]{:S(2)}, u32[]{:S(2)}) collective-permute-start(bf16[2,512,256]{2,1,0:T(8,128)(2,1)S(1)} %pad_maximum_fusion.23), channel_id=1, source_target_pairs={{0,16},{8,24},{16,0},{24,8},{1,17},{9,25},{17,1},{25,9},{2,18},{10... | collective-permute-start | bytes 1572872 | tf_op jit(solution)/shard_map/ppermute | solution.py:22
  618.4 35.7 %collective-permute-start.23 = (bf16[2,512,256]{2,1,0:T(8,128)(2,1)S(1)}, bf16[2,512,256]{2,1,0:T(8,128)(2,1)S(1)}, u32[]{:S(2)}, u32[]{:S(2)}) collective-permute-start(bf16[2,512,256]{2,1,0:T(8,128)(2,1)S(1)} %pad_maximum_fusion.24), channel_id=1, source_target_pairs={{0,16},{8,24},{16,0},{24,8},{1,17},{9,25},{17,1},{25,9},{2,18},{10... | collective-permute-start | bytes 1572872 | tf_op jit(solution)/shard_map/ppermute | solution.py:22
  657.3 64.6 %all-gather.34.cloned.1.call-start = ((), (), s32[]{:S(2)}) async-start(), calls=%async_computation.14 | async-start | bytes 2359296 | tf_op jit(solution)/shard_map/all_gather | solution.py:41
  687.6 8.5 %collective-permute-start.24 = (bf16[1,512,256]{2,1,0:T(8,128)(2,1)S(1)}, bf16[1,512,256]{2,1,0:T(8,128)(2,1)S(1)}, u32[]{:S(2)}, u32[]{:S(2)}) collective-permute-start(bf16[1,512,256]{2,1,0:T(8,128)(2,1)S(1)} %fusion.13), channel_id=1, source_target_pairs={{0,8},{8,0},{16,24},{24,16},{1,9},{9,1},{17,25},{25,17},{2,10},{10... | collective-permute-start | bytes 786440 | tf_op jit(solution)/shard_map/ppermute | solution.py:22
  696.3 25.4 %collective-permute-start.25 = (bf16[2,512,256]{2,1,0:T(8,128)(2,1)S(1)}, bf16[2,512,256]{2,1,0:T(8,128)(2,1)S(1)}, u32[]{:S(2)}, u32[]{:S(2)}) collective-permute-start(bf16[2,512,256]{2,1,0:T(8,128)(2,1)S(1)} %pad_maximum_fusion.25), channel_id=1, source_target_pairs={{0,16},{8,24},{16,0},{24,8},{1,17},{9,25},{17,1},{25,9},{2,18},{10... | collective-permute-start | bytes 1572872 | tf_op jit(solution)/shard_map/ppermute | solution.py:22
  698.8 23.1 %copy-start.7 = (f32[512,256]{1,0:T(8,128)S(1)}, f32[512,256]{1,0:T(8,128)}, u32[]{:S(2)}) copy-start(f32[512,256]{1,0:T(8,128)} %reduce-scatter.5.cloned.1.call-done) | copy-start | bytes 1572868
  (3 other events, 10.1 us)
Sparse Core Ops, SparseCore 0:
  26.2 118.6 reduce-scatter.2
  147.2 44.6 reduce-scatter.4
  196.1 28.6 all-gather.13
  226.6 28.0 all-gather.15
  257.0 28.2 all-gather.19
  346.4 27.0 all-gather.23
  376.0 28.0 all-gather.17
  406.0 28.0 all-gather.25
  455.5 27.9 all-gather.29
  485.8 28.0 all-gather.21
  515.9 28.0 all-gather.31
  546.3 28.0 all-gather.27
  576.3 28.0 all-gather.35
  657.4 27.8 all-gather.37
  687.6 28.0 all-gather.33
